TPU v7x, 32 devices: a whole 2x2x4 slice. The times are simulated.
32 devices in a mesh: ctx: 8 (over z, y), head: 4 (over x, core).
Axes of the slice: x: 2, y: 2, z: 4, core: 2. Of those that a mesh axis runs over, the one named last changes fastest.
Arguments:
- block_order: int32 [16], replicated, may hold values from 0 to 15, as said below
- main_query: bfloat16 [1024, 36864], P('ctx', 'head'), may hold values from -256 to 256
- latent_key: bfloat16 [576, 1024], P(None, 'ctx'), may hold values from -24 to 24
- index_query: bfloat16 [1024, 32, 128], P('ctx', 'head'), may hold values from -64 to 64
- index_weight: bfloat16 [1024, 32], P('ctx', 'head'), may hold values from -0.6 to 0.6
- index_key: bfloat16 [128, 1024], P(None, 'ctx'), may hold values from -24 to 24
Outputs:
- row_loss: float32 [1024], P('ctx')
- grad_query: bfloat16 [1024, 32, 128], P('ctx', 'head')
- grad_weight: bfloat16 [1024, 32], P('ctx', 'head')
- grad_key: float32 [1024, 128], P(('ctx', 'head'))
Inputs may be any that keep to these rules, and one draw needn't show every extreme that they name: `block_order`: slots 2d and 2d+1 hold blocks s * 8 + c and s * 8 + 16 // 2 - 1 - c of one sequence s, for some c below 4, and every block appears once.
All inputs are finite; a program needn't handle non-finite values.
Results may differ from a plain program's by a relative error of at most 0.01.
Values may be sent and summed in bfloat16 or wider, within the bound.
A program may use at most 128 MiB of HBM per device.

v0:
```python
import math

import jax
import jax.numpy as jnp
from jax import lax
from jax.sharding import PartitionSpec as P

HM = 64
HEAD_QK = 192
SEQS = 2


masked_value = -1e30


def pick_group(head_count, row_count):
    row_limit = max(256, row_count)
    chosen = 1
    for candidate in range(1, head_count + 1):
        if head_count % candidate == 0 and candidate * row_count <= row_limit:
            chosen = candidate
    return chosen


def window_start(row_pos, length):
    return row_pos[0] // length * length


def causal_target(queries, row_pos, key_rows, length):
    row_count = queries.shape[0]
    head_count = queries.shape[1]
    start_at = window_start(row_pos, length)
    window = lax.dynamic_slice_in_dim(key_rows, start_at, length, 1)
    key_pos = start_at + lax.iota(jnp.int32, length)
    visible = key_pos[None, :] <= row_pos[:, None]
    group_size = pick_group(head_count, row_count)
    score_scale = 1.0 / math.sqrt(HEAD_QK)
    target = jnp.zeros((row_count, length), jnp.float32)
    for group_index in range(head_count // group_size):
        grouped = queries[:, group_index * group_size : (group_index + 1) * group_size, :]
        scores = (
            jnp.einsum("rhk,ks->hrs", grouped, window, preferred_element_type=jnp.float32)
            * score_scale
        )
        scores = jnp.where(visible[None], scores, masked_value)
        top_score = jnp.max(scores, axis=2, keepdims=True)
        raised = jnp.exp(scores - top_score)
        target = target + jnp.sum(raised / jnp.sum(raised, axis=2, keepdims=True), axis=0)
    return (target * (1.0 / HM), start_at)


def index_scores(index_rows, index_weights, row_pos, key_rows, length):
    row_count = index_rows.shape[0]
    head_count = index_rows.shape[1]
    start_at = window_start(row_pos, length)
    window = lax.dynamic_slice_in_dim(key_rows, start_at, length, 1)
    key_pos = start_at + lax.iota(jnp.int32, length)
    visible = key_pos[None, :] <= row_pos[:, None]
    weights = index_weights.astype(jnp.float32)
    group_size = pick_group(head_count, row_count)
    logits = jnp.zeros((row_count, length), jnp.float32)
    for group_index in range(head_count // group_size):
        lower = group_index * group_size
        upper = lower + group_size
        activation = jnp.einsum(
            "rjd,ds->rjs", index_rows[:, lower:upper, :], window, preferred_element_type=jnp.float32
        )
        logits = logits + jnp.sum(
            jnp.maximum(activation, 0.0) * weights[:, lower:upper, None], axis=1
        )
    return jnp.where(visible, logits, 0.0)


def index_backward(index_rows, index_weights, row_pos, key_rows, slope_window, length):
    row_count = index_rows.shape[0]
    head_count = index_rows.shape[1]
    head_width = index_rows.shape[2]
    start_at = window_start(row_pos, length)
    window = lax.dynamic_slice_in_dim(key_rows, start_at, length, 1)
    weights = index_weights.astype(jnp.float32)
    slope_float = slope_window.astype(jnp.float32)
    group_size = pick_group(head_count, row_count)
    rows_parts = []
    weight_parts = []
    window_grad = jnp.zeros((length, head_width), jnp.float32)
    for group_index in range(head_count // group_size):
        lower = group_index * group_size
        upper = lower + group_size
        group_rows = index_rows[:, lower:upper, :]
        activation = jnp.einsum(
            "rjd,ds->rjs", group_rows, window, preferred_element_type=jnp.float32
        )
        weight_parts.append(jnp.sum(slope_float[:, None, :] * jnp.maximum(activation, 0.0), axis=2))
        through = jnp.where(
            activation > 0.0, slope_float[:, None, :] * weights[:, lower:upper, None], 0.0
        ).astype(jnp.bfloat16)
        rows_parts.append(
            jnp.einsum("rjs,ds->rjd", through, window, preferred_element_type=jnp.float32)
        )
        window_grad = window_grad + jnp.einsum(
            "rjs,rjd->sd", through, group_rows, preferred_element_type=jnp.float32
        )
    return (
        jnp.concatenate(rows_parts, axis=1),
        jnp.concatenate(weight_parts, axis=1),
        window_grad,
        start_at,
    )


def forward_items(main_rows, index_rows, index_weights, positions, sorted_latent, sorted_index):
    row_count = main_rows.shape[1]
    key_width = sorted_latent.shape[0]
    head_count = main_rows.shape[2] // key_width
    length = sorted_latent.shape[1] // SEQS
    queries = main_rows[0].reshape(row_count, head_count, key_width)
    target, start_at = causal_target(queries, positions[0], sorted_latent, length)
    targets = [target]
    starts = [start_at]
    logits_all = [index_scores(index_rows[0], index_weights[0], positions[0], sorted_index, length)]
    return (jnp.stack(targets), jnp.stack(logits_all), jnp.stack(starts))


def backward_items(index_rows, index_weights, positions, sorted_index, slope_windows, key_grad):
    length = slope_windows.shape[2]
    grad_rows, grad_weights, window_grad, start_at = index_backward(
        index_rows[0], index_weights[0], positions[0], sorted_index, slope_windows[0], length
    )
    key_grad = lax.dynamic_update_slice_in_dim(key_grad, window_grad, start_at, 0)
    grads_rows = [grad_rows]
    grads_weights = [grad_weights]
    return (jnp.stack(grads_rows), jnp.stack(grads_weights), key_grad)


def row_softmax(target, logits, positions, starts):
    length = logits.shape[2]
    key_pos = starts[:, None, None] + lax.iota(jnp.int32, length)[None, None, :]
    visible = key_pos <= positions[:, :, None]
    masked = jnp.where(visible, logits, masked_value)
    top_logit = jnp.max(masked, axis=2)
    total_exp = jnp.sum(jnp.where(visible, jnp.exp(masked - top_logit[:, :, None]), 0.0), axis=2)
    log_total = top_logit + jnp.log(total_exp)
    row_loss = jnp.sum(target, axis=2) * log_total - jnp.sum(target * logits, axis=2)
    slopes = jnp.where(visible, jnp.exp(masked - log_total[:, :, None]) - target, 0.0).astype(
        jnp.bfloat16
    )
    return (row_loss, lax.optimization_barrier(slopes))


def rows_work(
    main_rows, index_rows, index_weights, positions, sorted_latent, sorted_index, key_grad
):
    target, logits, starts = forward_items(
        main_rows, index_rows, index_weights, positions, sorted_latent, sorted_index
    )
    row_loss, slopes = row_softmax(target, logits, positions, starts)
    grad_rows, grad_weights, key_grad = backward_items(
        index_rows, index_weights, positions, sorted_index, slopes, key_grad
    )
    return (row_loss, grad_rows.astype(jnp.bfloat16), grad_weights.astype(jnp.bfloat16), key_grad)


def body(block_order, main_query, latent_key, index_query, index_weight, index_key):
    ctx_count = lax.axis_size("ctx")
    head_axis = lax.axis_size("head")
    local_rows = main_query.shape[0]
    block_rows = local_rows // 2
    seq_len = local_rows * ctx_count
    block_total = 2 * ctx_count
    key_width = latent_key.shape[0]
    index_width = index_key.shape[0]
    my_blocks = lax.dynamic_slice_in_dim(block_order, 2 * lax.axis_index("ctx"), 2, 0)
    slot_of = jnp.argsort(block_order)
    local_pos = my_blocks[:, None] * block_rows + lax.iota(jnp.int32, block_rows)[None, :]
    all_latent, all_index = (
        lax.all_gather(latent_key, "ctx", axis=1, tiled=True),
        lax.all_gather(index_key, "ctx", axis=1, tiled=True),
    )
    sorted_latent = all_latent.reshape(key_width, block_total, block_rows)[:, slot_of, :].reshape(
        key_width, seq_len
    )
    sorted_index = all_index.reshape(index_width, block_total, block_rows)[:, slot_of, :].reshape(
        index_width, seq_len
    )
    key_grad = jnp.zeros((seq_len, index_width), jnp.float32)
    main_rows, index_rows, index_weights = (
        lax.all_to_all(main_query, "head", split_axis=0, concat_axis=1, tiled=True),
        lax.all_to_all(index_query, "head", split_axis=0, concat_axis=1, tiled=True),
        lax.all_to_all(index_weight, "head", split_axis=0, concat_axis=1, tiled=True),
    )
    part_rows = local_rows // head_axis
    positions = lax.dynamic_slice_in_dim(
        local_pos.reshape(local_rows), lax.axis_index("head") * part_rows, part_rows, 0
    )[None, :]
    row_loss, grad_rows, grad_weights, key_grad = rows_work(
        main_rows[None],
        index_rows[None],
        index_weights[None],
        positions,
        sorted_latent,
        sorted_index,
        key_grad,
    )
    grad_query, grad_weight = (
        lax.all_to_all(grad_rows[0], "head", split_axis=1, concat_axis=0, tiled=True),
        lax.all_to_all(grad_weights[0], "head", split_axis=1, concat_axis=0, tiled=True),
    )
    loss_rows = lax.all_gather(row_loss[0], "head", axis=0, tiled=True)
    stored_grad = key_grad.reshape(block_total, block_rows, index_width)[block_order].reshape(
        seq_len, index_width
    )
    grad_key = lax.psum_scatter(stored_grad, ("ctx", "head"), scatter_dimension=0, tiled=True)
    return (loss_rows, grad_query, grad_weight, grad_key)


def solution(mesh):
    in_specs = (
        P(),
        P("ctx", "head"),
        P(None, "ctx"),
        P("ctx", "head", None),
        P("ctx", "head"),
        P(None, "ctx"),
    )
    out_specs = (P("ctx"), P("ctx", "head", None), P("ctx", "head"), P(("ctx", "head"), None))
    return jax.shard_map(body, mesh=mesh, in_specs=in_specs, out_specs=out_specs, check_vma=False)
```

profile of v0, /device:TPU:0, one launch (start us, length us, event | category | flops | bytes accessed | tf_op | source)
XLA Modules:
  0.0 269.8 jit_solution(10024266576849094286)
XLA Ops:
  7.2 1.7 copy.79
  10.4 4.2 %all-to-all-start.2 = ((bf16[4,2,128]{2,1,0:T(2,128)(2,1)}), bf16[4,2,128]{2,1,0:T(2,128)(2,1)S(1)}, u32[]{:S(2)}, u32[]{:S(2)}) async-start(bf16[4,2,128]{2,1,0:T(2,128)(2,1)} %reshape.641), calls=%async_computation.2 | async-start | bytes 4096 | tf_op jit(solution)/shard_map/all_to_all | solution.py:189
  16.4 1.9 sort.17
  18.4 0.9 copy.90
  19.2 32.0 %all_gather.10 = bf16[128,1024]{0,1:T(8,128)(2,1)S(1)} all-gather(bf16[128,128]{0,1:T(8,128)(2,1)S(1)} %copy.90), channel_id=1, replica_groups=mesh['ctx'=8,'head'=4] {'ctx'}, dimensions={1}, use_global_device_ids=true | all-gather | bytes 294912 | tf_op jit(solution)/shard_map/all_gather | solution.py:177
  53.7 3.4 %all-to-all-start.1 = ((bf16[128,8,128]{2,1,0:T(8,128)(2,1)}), bf16[128,8,128]{2,1,0:T(8,128)(2,1)S(1)}, u32[]{:S(2)}, u32[]{:S(2)}) async-start(bf16[128,8,128]{2,1,0:T(8,128)(2,1)} %param.9), calls=%async_computation.1 | async-start | bytes 524288 | tf_op jit(solution)/shard_map/all_to_all | solution.py:188
  57.3 5.8 %all-to-all-done.1 = bf16[128,8,128]{2,1,0:T(8,128)(2,1)S(1)} async-done(((bf16[128,8,128]{2,1,0:T(8,128)(2,1)}), bf16[128,8,128]{2,1,0:T(8,128)(2,1)S(1)}, u32[]{:S(2)}, u32[]{:S(2)}) %all-to-all-start.1) | async-done | bytes 262176 | tf_op jit(solution)/shard_map/all_to_all | solution.py:188
  63.1 3.6 %all-to-all-start = ((bf16[4,32,9216]{2,1,0:T(8,128)(2,1)}), bf16[4,32,9216]{2,1,0:T(8,128)(2,1)S(1)}, u32[]{:S(2)}, u32[]{:S(2)}) async-start(bf16[4,32,9216]{2,1,0:T(8,128)(2,1)} %bitcast.393), calls=%async_computation | async-start | bytes 4718592 | tf_op jit(solution)/shard_map/all_to_all | solution.py:187
  67.2 1.0 fusion.74
  68.2 1.1 fusion.72
  69.2 1.0 fusion.68
  71.2 24.0 %all-to-all-done = bf16[4,32,9216]{2,1,0:T(8,128)(2,1)S(1)} async-done(((bf16[4,32,9216]{2,1,0:T(8,128)(2,1)}), bf16[4,32,9216]{2,1,0:T(8,128)(2,1)S(1)}, u32[]{:S(2)}, u32[]{:S(2)}) %all-to-all-start) | async-done | bytes 2359328 | tf_op jit(solution)/shard_map/all_to_all | solution.py:187
  95.2 3.3 %copy.81 = bf16[32,4,9216]{2,1,0:T(4,128)(2,1)} copy(bf16[32,4,9216]{2,0,1:T(8,128)(2,1)S(1)} %bitcast.375) | data formatting | bytes 4718592 | tf_op jit(solution)/shard_map/all_to_all | solution.py:187
  98.5 4.5 %reshape_squeeze_broadcast_in_dim.3 = bf16[32,64,576]{2,1,0:T(8,128)(2,1)S(1)} reshape(bf16[32,4,9216]{2,1,0:T(4,128)(2,1)} %copy.81) | data formatting | bytes 4718592 | tf_op jit(solution)/shard_map/reshape;squeeze;broadcast_in_dim | solution.py:116
  103.0 1.6 fusion.376
  104.6 2.1 gather_fusion
  106.7 1.6 fusion.378
  108.2 1.6 fusion.383
  109.8 1.6 fusion.388
  111.4 1.6 fusion.393
  112.9 1.6 fusion.398
  114.5 2.2 fusion.403
  116.7 2.2 fusion.408
  118.9 2.3 fusion.413
  121.2 1.0 fusion.109
  122.2 1.7 fusion.75
  125.3 1.5 gather_fusion.2
  127.6 3.2 %all-to-all-start.4 = ((bf16[4,2,128]{2,1,0:T(2,128)(2,1)}), bf16[4,2,128]{2,1,0:T(2,128)(2,1)S(1)}, u32[]{:S(2)}, u32[]{:S(2)}) async-start(bf16[4,2,128]{2,1,0:T(2,128)(2,1)} %reshape.643), calls=%async_computation.4 | async-start | bytes 4096 | tf_op jit(solution)/shard_map/all_to_all | solution.py:206
  132.8 8.1 %all-reduce = f32[128]{0:T(128)} all-reduce(f32[128]{0:T(128)S(1)} %subtract_dynamic-update-slice_fusion), channel_id=1, replica_groups=mesh['ctx'=8,'head'=4] {'head'}, use_global_device_ids=true, to_apply=%add | all-reduce | flops 128 | bytes 1024
  140.9 3.4 %all-to-all-start.3 = ((bf16[32,32,128]{2,0,1:T(8,128)(2,1)}), bf16[32,32,128]{2,0,1:T(8,128)(2,1)S(1)}, u32[]{:S(2)}, u32[]{:S(2)}) async-start(bf16[32,32,128]{2,0,1:T(8,128)(2,1)} %copy.98), calls=%async_computation.3 | async-start | bytes 524288 | tf_op jit(solution)/shard_map/all_to_all | solution.py:205
  145.1 5.3 %all-to-all-done.3 = bf16[32,32,128]{2,0,1:T(8,128)(2,1)S(1)} async-done(((bf16[32,32,128]{2,0,1:T(8,128)(2,1)}), bf16[32,32,128]{2,0,1:T(8,128)(2,1)S(1)}, u32[]{:S(2)}, u32[]{:S(2)}) %all-to-all-start.3) | async-done | bytes 262176 | tf_op jit(solution)/shard_map/all_to_all | solution.py:205
  151.2 111.8 %reduce-scatter.2.cloned.1.call-done = f32[32,128]{1,0:T(8,128)} async-done(((f32[1024,128]{1,0:T(8,128)}), f32[32,128]{1,0:T(8,128)}) %reduce-scatter.2.cloned.1.call-update) | async-done | bytes 16400 | tf_op jit(solution)/shard_map/reduce_scatter | solution.py:212
  (75 shorter events, 12.0 us)
Async XLA Ops:
  7.2 45.3 %copy-start.10 = (u32[32]{0:T(128)S(1)}, u32[32]{0:T(128)}, u32[]{:S(2)}) copy-start(u32[32]{0:T(128)} %constant.59) | copy-start | bytes 388
  7.2 97.4 %all-gather.2.cloned.1.call-start = ((), (), s32[]{:S(2)}) async-start(), calls=%async_computation.6 | async-start | bytes 1474560 | tf_op jit(solution)/shard_map/all_gather | solution.py:176
  10.4 43.3 %all-to-all-start.2 = ((bf16[4,2,128]{2,1,0:T(2,128)(2,1)}), bf16[4,2,128]{2,1,0:T(2,128)(2,1)S(1)}, u32[]{:S(2)}, u32[]{:S(2)}) async-start(bf16[4,2,128]{2,1,0:T(2,128)(2,1)} %reshape.641), calls=%async_computation.2 | async-start | bytes 4096 | tf_op jit(solution)/shard_map/all_to_all | solution.py:189
  15.6 54.9 %copy-start.5 = (s32[32]{0:T(128)}, s32[32]{0:T(128)S(1)}, u32[]{:S(2)}) copy-start(s32[32]{0:T(128)S(1)} %dynamic_slice.14) | copy-start | bytes 388
  53.7 9.4 %all-to-all-start.1 = ((bf16[128,8,128]{2,1,0:T(8,128)(2,1)}), bf16[128,8,128]{2,1,0:T(8,128)(2,1)S(1)}, u32[]{:S(2)}, u32[]{:S(2)}) async-start(bf16[128,8,128]{2,1,0:T(8,128)(2,1)} %param.9), calls=%async_computation.1 | async-start | bytes 524288 | tf_op jit(solution)/shard_map/all_to_all | solution.py:188
  57.2 54.1 %copy-start.7 = (pred[32,512]{1,0:T(8,128)(4,1)}, pred[32,512]{1,0:T(8,128)(4,1)S(1)}, u32[]{:S(2)}) copy-start(pred[32,512]{1,0:T(8,128)(4,1)S(1)} %broadcast_compare_fusion) | copy-start | bytes 49156
  63.1 32.1 %all-to-all-start = ((bf16[4,32,9216]{2,1,0:T(8,128)(2,1)}), bf16[4,32,9216]{2,1,0:T(8,128)(2,1)S(1)}, u32[]{:S(2)}, u32[]{:S(2)}) async-start(bf16[4,32,9216]{2,1,0:T(8,128)(2,1)} %bitcast.393), calls=%async_computation | async-start | bytes 4718592 | tf_op jit(solution)/shard_map/all_to_all | solution.py:187
  66.8 196.2 %reduce-scatter.2.cloned.1.call-start = ((), (), s32[]{:S(2)}) async-start(), calls=%async_computation.7 | async-start | bytes 540672 | tf_op jit(solution)/shard_map/reduce_scatter | solution.py:212
  66.8 2.4 copy-start.4
  66.9 3.4 %copy-start.2 = (bf16[4,32,8,128]{3,1,2,0:T(8,128)(2,1)}, bf16[4,32,8,128]{3,1,2,0:T(8,128)(2,1)S(1)}, u32[]{:S(2)}) copy-start(bf16[4,32,8,128]{3,1,2,0:T(8,128)(2,1)S(1)} %copy.92) | copy-start | bytes 786436
  112.9 1.6 copy-start.8
  118.9 3.3 %copy-start = (f32[512,32,8]{0,1,2:T(8,128)S(1)}, f32[512,32,8]{0,1,2:T(8,128)}, u32[]{:S(2)}) copy-start(f32[512,32,8]{0,1,2:T(8,128)} %get-tuple-element.37) | copy-start | bytes 1572868
  118.9 3.3 %copy-start.1 = (f32[512,32,8]{0,1,2:T(8,128)S(1)}, f32[512,32,8]{0,1,2:T(8,128)}, u32[]{:S(2)}) copy-start(f32[512,32,8]{0,1,2:T(8,128)} %get-tuple-element.39) | copy-start | bytes 1572868
  122.2 1.7 copy-start.3
  125.1 5.7 %copy-start.6 = (s32[32]{0:T(128)S(1)}, s32[32]{0:T(128)}, u32[]{:S(2)}) copy-start(s32[32]{0:T(128)} %copy-done.5) | copy-start | bytes 388
  125.1 5.9 %copy-start.9 = (f32[32]{0:T(128)S(1)}, f32[32]{0:T(128)}, u32[]{:S(2)}) copy-start(f32[32]{0:T(128)} %log_add_fusion) | copy-start | bytes 388
  127.6 13.4 %all-to-all-start.4 = ((bf16[4,2,128]{2,1,0:T(2,128)(2,1)}), bf16[4,2,128]{2,1,0:T(2,128)(2,1)S(1)}, u32[]{:S(2)}, u32[]{:S(2)}) async-start(bf16[4,2,128]{2,1,0:T(2,128)(2,1)} %reshape.643), calls=%async_computation.4 | async-start | bytes 4096 | tf_op jit(solution)/shard_map/all_to_all | solution.py:206
  140.9 9.5 %all-to-all-start.3 = ((bf16[32,32,128]{2,0,1:T(8,128)(2,1)}), bf16[32,32,128]{2,0,1:T(8,128)(2,1)S(1)}, u32[]{:S(2)}, u32[]{:S(2)}) async-start(bf16[32,32,128]{2,0,1:T(8,128)(2,1)} %copy.98), calls=%async_computation.3 | async-start | bytes 524288 | tf_op jit(solution)/shard_map/all_to_all | solution.py:205
Sparse Core Ops, SparseCore 0:
  10.2 45.9 all-gather.1
  127.0 135.9 reduce-scatter.1
where the time goes:
time: 271 us; the launch traced here: 270 us
  waiting for transfers between devices  147 us (54%)
  blocking collectives  40.2 us (15%)
  local copies, waits for them, and re-layouts  21.6 us (8%)
  matrix products  19.9 us (7%)
  starting transfers between devices  18 us (7%)
  between operations  15.3 us (6%)
  other arithmetic  8.01 us (3%)
    reduce_scatter x1, waiting for transfers between devices, body(): lax.psum_scatter(stored_grad, ('ctx', 'head'), scatter_dimension=0, tiled...  112 us
    all_gather x1, blocking collectives, body(): lax.all_gather(index_key, 'ctx', axis=1, tiled=True)  32 us
    all_to_all x1, waiting for transfers between devices, body(): lax.all_to_all(main_query, 'head', split_axis=0, concat_axis=1, tiled=True)  24 us
    div x8, matrix products, causal_target(): raised / jnp.sum(raised, axis=2, keepdims=True)  14.4 us
    unnamed x1, blocking collectives  8.12 us
    all_to_all x1, waiting for transfers between devices, body(): lax.all_to_all(index_query, 'head', split_axis=0, concat_axis=1, tiled=True)  5.79 us
  transfers between devices with their start and end apart: 7, of which 4 were waited for; matrix products, arithmetic and copies ran while one was open for 9% of the time, Pallas kernels for 0%

commit v1 on v0

v1 whole, which is shorter than its diff:
```python
import functools
import math

import jax
import jax.numpy as jnp
from jax import lax
from jax.experimental import pallas as pl
from jax.experimental.pallas import tpu as pltpu
from jax.sharding import PartitionSpec as P

HEAD_QK = 192
LANES = 128
HALF = 64
masked_value = -1e30


def each(lower, upper, step):
    if upper - lower <= 16:
        for index in range(lower, upper):
            step(index)
    else:
        lax.fori_loop(lower, upper, lambda index, carry: (step(index), carry)[1], 0)


def total_over(upper, term):
    if upper <= 16:
        return functools.reduce(lambda a, b: a + b, [term(index) for index in range(upper)])
    return lax.fori_loop(0, upper, lambda index, carry: carry + term(index), jnp.int32(0))


def dot(a, b):
    return jnp.dot(a, b, preferred_element_type=jnp.float32)


def kernel(
    dims,
    order_ref,
    query_ref,
    latent_ref,
    rows_ref,
    weight_ref,
    index_ref,
    loss_ref,
    grad_rows_ref,
    grad_weight_ref,
    grad_key_ref,
    query_vmem,
    all_latent,
    all_index,
    window_latent,
    window_index,
    rows_turned,
    weight_col,
    act_early,
    act_late,
    part_logit,
    part_target,
    got_logit,
    got_target,
    slopes,
    losses,
    weight_grads,
    key_turned,
    key_parts,
    got_key,
    key_piece,
    key_send,
    got_piece,
    query_sem,
    index_send,
    index_recv,
    latent_send,
    latent_recv,
    logit_send,
    logit_recv,
    target_send,
    target_recv,
    slope_send,
    slope_recv,
    loss_send,
    loss_recv,
    key_send_sem,
    key_recv_sem,
    piece_send,
    piece_recv,
):
    ctx_count, head_axis, block_rows, heads, width, index_heads = dims
    pairs = ctx_count // 2
    length = ctx_count * block_rows
    early = length // 2
    quarter = block_rows // head_axis
    me = lax.axis_index("ctx")
    head = lax.axis_index("head")
    across = (head + 2) % 4
    beside = head + 1 - 2 * (head % 2)

    fetch_query = pltpu.make_async_copy(query_ref, query_vmem, query_sem)
    fetch_query.start()

    barrier = pltpu.get_barrier_semaphore()

    def greet_ctx(offset):
        pl.semaphore_signal(
            barrier, inc=1, device_id={"ctx": (me + offset) % ctx_count}, device_id_type=pl.DeviceIdType.MESH
        )

    def greet_head(offset):
        pl.semaphore_signal(
            barrier, inc=1, device_id={"head": (head + offset) % head_axis}, device_id_type=pl.DeviceIdType.MESH
        )

    each(1, ctx_count, greet_ctx)
    each(1, head_axis, greet_head)
    pl.semaphore_wait(barrier, ctx_count - 1 + head_axis - 1)

    def send(source, target, send_sem, recv_sem, where):
        return pltpu.make_async_remote_copy(
            src_ref=source,
            dst_ref=target,
            send_sem=send_sem,
            recv_sem=recv_sem,
            device_id=where,
            device_id_type=pl.DeviceIdType.MESH,
        )

    def keys_plan(own_ref, all_ref, sends, recvs):
        depth = own_ref.shape[0] // head_axis

        def piece(owner, quarter_index):
            return all_ref.at[owner, pl.ds(pl.multiple_of(quarter_index * depth, 16), depth), :]

        def first(offset):
            mine = own_ref.at[pl.ds(pl.multiple_of(head * depth, 16), depth), :]
            return send(
                mine, piece(me, head), sends.at[0, offset], recvs.at[0, offset], {"ctx": (me + offset) % ctx_count}
            )

        def onward(stage, offset):
            owner = (me + ctx_count - offset) % ctx_count
            which = across if stage == 3 else head
            where = {"head": across} if stage == 1 else {"head": beside}
            return send(
                piece(owner, which), piece(owner, which), sends.at[stage, offset], recvs.at[stage, offset], where
            )

        return first, onward

    index_first, index_onward = keys_plan(index_ref, all_index, index_send, index_recv)
    latent_first, latent_onward = keys_plan(latent_ref, all_latent, latent_send, latent_recv)
    each(1, ctx_count, lambda k: index_first(k).start())
    each(1, ctx_count, lambda k: latent_first(k).start())

    all_index[me] = index_ref[...]
    all_latent[me] = latent_ref[...]

    sequence = order_ref[2 * me] // ctx_count
    inner = order_ref[2 * me] % ctx_count

    def holder(pair):
        wanted = sequence * ctx_count + pair
        found = total_over(
            ctx_count, lambda d: jnp.where(order_ref[2 * d] == wanted, jnp.int32(1), jnp.int32(0)) * d
        )
        return jnp.minimum(found, ctx_count - 1)

    flat_rows = 2 * block_rows * index_heads
    rows_turned[...] = rows_ref[...].T
    spread = (
        lax.broadcasted_iota(jnp.int32, (flat_rows, 2 * block_rows), 0) // index_heads
        == lax.broadcasted_iota(jnp.int32, (flat_rows, 2 * block_rows), 1)
    ).astype(jnp.bfloat16)
    spread_weight = lax.dot_general(
        spread, weight_ref[...], (((1,), (1,)), ((), ())), preferred_element_type=jnp.float32
    )
    own_lane = lax.broadcasted_iota(
        jnp.int32, (flat_rows, index_heads), 0
    ) % index_heads == lax.broadcasted_iota(jnp.int32, (flat_rows, index_heads), 1)
    weight_col[...] = jnp.broadcast_to(
        jnp.sum(jnp.where(own_lane, spread_weight, 0.0), axis=1, keepdims=True), (flat_rows, LANES)
    )
    window_latent[0:HALF, :] = jnp.zeros((HALF, length), jnp.bfloat16)
    window_latent[HALF + width :, :] = jnp.zeros((HALF, length), jnp.bfloat16)

    def forward(onward):
        def one(offset):
            onward(0, offset).wait_recv()
            onward(1, offset).start()
            onward(2, offset).start()

        def two(offset):
            onward(1, offset).wait_recv()
            onward(3, offset).start()

        def three(offset):
            onward(2, offset).wait_recv()
            onward(3, offset).wait_recv()

        each(1, ctx_count, one)
        each(1, ctx_count, two)
        each(1, ctx_count, three)

    def arrange(all_ref, window_ref, top, depth):
        for pair in range(0, pairs, 2):
            a = all_ref[holder(pair)]
            b = all_ref[holder(pair + 1)]
            low = pair * block_rows
            high = length - (pair + 2) * block_rows
            window_ref[top : top + depth, low : low + LANES] = jnp.concatenate([a[:, :HALF], b[:, :HALF]], axis=1)
            window_ref[top : top + depth, high : high + LANES] = jnp.concatenate([b[:, HALF:], a[:, HALF:]], axis=1)

    chunk_rows = 16
    flat = chunk_rows * index_heads
    chunks = block_rows // chunk_rows
    sides = ((0, early, 0, act_early), (1, length, early, act_late))

    def logits_of():
        for side, columns, column_at, act_ref in sides:

            def chunk(i, carry):
                local = pl.multiple_of(i * flat, flat)
                at = pl.multiple_of(side * block_rows * index_heads + i * flat, flat)
                act = dot(rows_ref[pl.ds(at, flat), :], window_index[:, 0:columns])
                act_ref[pl.ds(local, flat), :] = act
                scaled = jnp.maximum(act, 0.0) * weight_col[pl.ds(at, flat), 0:1]
                part_logit[pl.ds(pl.multiple_of(i * chunk_rows, chunk_rows), chunk_rows), column_at : column_at + columns] = (
                    jnp.sum(scaled.reshape(chunk_rows, index_heads, columns), axis=1)
                )
                return carry

            lax.fori_loop(0, chunks, chunk, 0)

    def visible_of(side, rows, row_at, columns):
        block = jnp.where(side == 0, inner, ctx_count - 1 - inner)
        row_pos = block * block_rows + row_at + lax.broadcasted_iota(jnp.int32, (rows, columns), 0)
        return lax.broadcasted_iota(jnp.int32, (rows, columns), 1) <= row_pos

    def share(part_ref, got_ref, sends, recvs, offset):
        peer = (head + offset) % head_axis
        return send(
            part_ref.at[pl.ds(pl.multiple_of(peer * quarter, quarter), quarter), :],
            got_ref.at[offset],
            sends.at[offset],
            recvs.at[offset],
            {"head": peer},
        )

    score_scale = 1.0 / math.sqrt(HEAD_QK)
    group = max(1, min(heads // 2, 2048 // length))
    groups = heads // 2 // group
    padded = width + HALF

    def attention():
        part_target[...] = jnp.zeros(part_target.shape, jnp.float32)
        for parity in range(2):
            top = HALF if parity == 0 else 0
            lane_at = 0 if parity == 0 else width - HALF
            for side, columns, column_at, unused in sides:
                visible = visible_of(side, block_rows, 0, columns)

                def run(i, carry):
                    stacked = jnp.concatenate(
                        [
                            query_vmem[
                                side * block_rows : (side + 1) * block_rows,
                                pl.ds(pl.multiple_of((i * group + g) * 2 * width + lane_at, LANES), padded),
                            ]
                            for g in range(group)
                        ],
                        axis=0,
                    )
                    scores = dot(stacked, window_latent[top : top + padded, 0:columns]) * score_scale
                    total = part_target[:, column_at : column_at + columns]
                    for g in range(group):
                        one = jnp.where(visible, scores[g * block_rows : (g + 1) * block_rows], masked_value)
                        raised = jnp.exp(one - jnp.max(one, axis=1, keepdims=True))
                        total = total + raised * (1.0 / jnp.sum(raised, axis=1, keepdims=True))
                    part_target[:, column_at : column_at + columns] = total
                    return carry

                lax.fori_loop(0, groups, run, 0)

    forward(index_onward)
    arrange(all_index, window_index, 0, index_ref.shape[0])
    logits_of()
    each(1, head_axis, lambda k: share(part_logit, got_logit, logit_send, logit_recv, k).start())
    forward(latent_onward)
    arrange(all_latent, window_latent, HALF, width)
    fetch_query.wait()
    attention()
    each(1, head_axis, lambda k: share(part_target, got_target, target_send, target_recv, k).start())
    each(1, head_axis, lambda k: share(part_logit, got_logit, logit_send, logit_recv, k).wait_recv())
    each(1, head_axis, lambda k: share(part_target, got_target, target_send, target_recv, k).wait_recv())

    my_rows = pl.ds(pl.multiple_of(head * quarter, quarter), quarter)
    for side, columns, column_at, unused in sides:
        at = slice(column_at, column_at + columns)
        visible = visible_of(side, quarter, head * quarter, columns)
        logit = part_logit[my_rows, at]
        target = part_target[my_rows, at]
        for k in range(1, head_axis):
            logit = logit + got_logit[k, :, at]
            target = target + got_target[k, :, at]
        target = target * (1.0 / (heads * head_axis))
        masked = jnp.where(visible, logit, masked_value)
        top = jnp.max(masked, axis=1, keepdims=True)
        lse = top + jnp.log(jnp.sum(jnp.exp(masked - top), axis=1, keepdims=True))
        loss = jnp.sum(jnp.where(visible, target * (lse - logit), 0.0), axis=1, keepdims=True)
        slopes[my_rows, at] = jnp.where(visible, jnp.exp(masked - lse) - target, 0.0).astype(jnp.bfloat16)
        losses[head, side] = jnp.broadcast_to(loss, (quarter, LANES))

    def spread_slopes(offset):
        return send(
            slopes.at[my_rows, :],
            slopes.at[my_rows, :],
            slope_send.at[offset],
            slope_recv.at[offset],
            {"head": (head + offset) % head_axis},
        )

    def spread_losses(offset):
        return send(
            losses.at[head],
            losses.at[head],
            loss_send.at[offset],
            loss_recv.at[offset],
            {"head": (head + offset) % head_axis},
        )

    each(1, head_axis, lambda k: spread_slopes(k).start())
    each(1, head_axis, lambda k: spread_losses(k).start())
    each(1, head_axis, lambda k: spread_slopes(k).wait_recv())

    key_turned[...] = jnp.zeros(key_turned.shape, jnp.float32)
    lane_of = lax.broadcasted_iota(jnp.int32, (flat, LANES), 1)
    lane_own = lane_of == lax.broadcasted_iota(jnp.int32, (flat, LANES), 0) % index_heads
    for side, columns, column_at, act_ref in sides:

        def chunk(i, carry):
            local = pl.multiple_of(i * flat, flat)
            at = pl.multiple_of(side * block_rows * index_heads + i * flat, flat)
            rows_at = pl.multiple_of(i * chunk_rows, chunk_rows)
            act = act_ref[pl.ds(local, flat), :]
            slope = slopes[pl.ds(rows_at, chunk_rows), column_at : column_at + columns].astype(jnp.float32)
            slope = jnp.broadcast_to(slope[:, None, :], (chunk_rows, index_heads, columns)).reshape(flat, columns)
            col = jnp.sum(slope * jnp.maximum(act, 0.0), axis=1, keepdims=True)
            placed = jnp.where(lane_own, col, 0.0).reshape(chunk_rows, index_heads, LANES)
            weight_at = pl.multiple_of(side * block_rows + i * chunk_rows, chunk_rows)
            weight_grads[pl.ds(weight_at, chunk_rows), :] = jnp.sum(placed, axis=1)
            through = jnp.where(act > 0.0, slope * weight_col[pl.ds(at, flat), 0:1], 0.0).astype(jnp.bfloat16)
            grad_rows_ref[pl.ds(at, flat), :] = lax.dot_general(
                through,
                window_index[:, 0:columns],
                (((1,), (1,)), ((), ())),
                preferred_element_type=jnp.float32,
            ).astype(jnp.bfloat16)
            key_turned[:, 0:columns] += dot(rows_turned[:, pl.ds(at, flat)], through)
            return carry

        lax.fori_loop(0, chunks, chunk, 0)

    slot_rows = 2 * block_rows // head_axis
    grad_weight_ref[...] = weight_grads[...].T[0:index_heads].astype(jnp.bfloat16)
    for pair in range(pairs):
        low = pair * block_rows
        high = length - (pair + 1) * block_rows
        for part, start in ((0, low), (2, high)):
            lanes_at = start // LANES * LANES
            turned = key_turned[:, lanes_at : lanes_at + LANES].T
            for k in range(2):
                begin = start - lanes_at + k * slot_rows
                key_parts[part + k, pair] = turned[begin : begin + slot_rows]

    def share_key(offset):
        peer = (head + offset) % head_axis
        return send(
            key_parts.at[peer], got_key.at[offset], key_send_sem.at[offset], key_recv_sem.at[offset], {"head": peer}
        )

    each(1, head_axis, lambda k: share_key(k).start())
    each(1, head_axis, lambda k: spread_losses(k).wait_recv())
    loss_block = jnp.concatenate(
        [losses[q, side] for side in range(2) for q in range(head_axis)], axis=0
    )
    diagonal = lax.broadcasted_iota(jnp.int32, loss_block.shape, 0) == lax.broadcasted_iota(
        jnp.int32, loss_block.shape, 1
    )
    loss_ref[...] = jnp.sum(jnp.where(diagonal, loss_block, 0.0), axis=0, keepdims=True)
    each(1, head_axis, lambda k: share_key(k).wait_recv())
    for pair in range(pairs):
        piece = key_parts[head, pair]
        for k in range(1, head_axis):
            piece = piece + got_key[k, pair]
        key_piece[pair] = piece

    def fill(d):
        block = order_ref[2 * d]
        same = block // ctx_count == sequence
        key_send[d] = jnp.where(same, key_piece[block % ctx_count], 0.0)

    each(0, ctx_count, fill)

    def share_piece(offset):
        peer = (me + offset) % ctx_count
        return send(
            key_send.at[peer], got_piece.at[offset], piece_send.at[offset], piece_recv.at[offset], {"ctx": peer}
        )

    each(1, ctx_count, lambda k: share_piece(k).start())
    grad_key_ref[...] = key_send[me]

    def add(offset):
        share_piece(offset).wait_recv()
        grad_key_ref[...] += got_piece[offset]

    each(1, ctx_count, add)

    def finish_ctx(offset):
        index_first(offset).wait_send()
        latent_first(offset).wait_send()
        for stage in range(1, 4):
            index_onward(stage, offset).wait_send()
            latent_onward(stage, offset).wait_send()
        share_piece(offset).wait_send()

    def finish_head(offset):
        share(part_logit, got_logit, logit_send, logit_recv, offset).wait_send()
        share(part_target, got_target, target_send, target_recv, offset).wait_send()
        spread_slopes(offset).wait_send()
        spread_losses(offset).wait_send()
        share_key(offset).wait_send()

    each(1, ctx_count, finish_ctx)
    each(1, head_axis, finish_head)


def body(block_order, main_query, latent_key, index_query, index_weight, index_key):
    ctx_count = lax.axis_size("ctx")
    head_axis = lax.axis_size("head")
    local_rows = main_query.shape[0]
    block_rows = local_rows // 2
    width = latent_key.shape[0]
    heads = main_query.shape[1] // width
    index_heads, index_width = index_query.shape[1:]
    length = ctx_count * block_rows
    early = length // 2
    packed = early + length
    pairs = ctx_count // 2
    quarter = block_rows // head_axis
    slot_rows = local_rows // head_axis
    flat_rows = local_rows * index_heads
    f32, bf16 = jnp.float32, jnp.bfloat16
    vmem = pl.BlockSpec(memory_space=pltpu.VMEM)
    dma = pltpu.SemaphoreType.DMA
    loss, grad_rows, grad_weight, grad_key = pl.pallas_call(
        functools.partial(kernel, (ctx_count, head_axis, block_rows, heads, width, index_heads)),
        out_shape=(
            jax.ShapeDtypeStruct((1, local_rows), f32),
            jax.ShapeDtypeStruct((flat_rows, index_width), bf16),
            jax.ShapeDtypeStruct((index_heads, local_rows), bf16),
            jax.ShapeDtypeStruct((slot_rows, index_width), f32),
        ),
        in_specs=[
            pl.BlockSpec(memory_space=pltpu.SMEM),
            pl.BlockSpec(memory_space=pl.ANY),
            vmem,
            vmem,
            vmem,
            vmem,
        ],
        out_specs=(vmem, vmem, vmem, vmem),
        scratch_shapes=[
            pltpu.VMEM(main_query.shape, bf16),
            pltpu.VMEM((ctx_count,) + latent_key.shape, bf16),
            pltpu.VMEM((ctx_count,) + index_key.shape, bf16),
            pltpu.VMEM((width + 2 * HALF, length), bf16),
            pltpu.VMEM((index_width, length), bf16),
            pltpu.VMEM((index_width, flat_rows), bf16),
            pltpu.VMEM((flat_rows, LANES), f32),
            pltpu.VMEM((flat_rows // 2, early), f32),
            pltpu.VMEM((flat_rows // 2, length), f32),
            pltpu.VMEM((block_rows, packed), f32),
            pltpu.VMEM((block_rows, packed), f32),
            pltpu.VMEM((head_axis, quarter, packed), f32),
            pltpu.VMEM((head_axis, quarter, packed), f32),
            pltpu.VMEM((block_rows, packed), bf16),
            pltpu.VMEM((head_axis, 2, quarter, LANES), f32),
            pltpu.VMEM((local_rows, LANES), f32),
            pltpu.VMEM((index_width, length), f32),
            pltpu.VMEM((head_axis, pairs, slot_rows, index_width), f32),
            pltpu.VMEM((head_axis, pairs, slot_rows, index_width), f32),
            pltpu.VMEM((pairs, slot_rows, index_width), f32),
            pltpu.VMEM((ctx_count, slot_rows, index_width), f32),
            pltpu.VMEM((ctx_count, slot_rows, index_width), f32),
            dma,
            dma((4, ctx_count)),
            dma((4, ctx_count)),
            dma((4, ctx_count)),
            dma((4, ctx_count)),
        ]
        + [dma((head_axis,))] * 10
        + [dma((ctx_count,))] * 2,
        compiler_params=pltpu.CompilerParams(
            collective_id=0, has_side_effects=True, vmem_limit_bytes=60 * 1024 * 1024
        ),
    )(
        block_order,
        main_query,
        latent_key,
        index_query.reshape(flat_rows, index_width),
        index_weight.T,
        index_key,
    )
    return (
        loss.reshape(local_rows),
        grad_rows.reshape(local_rows, index_heads, index_width),
        grad_weight.T,
        grad_key,
    )


def solution(mesh):
    in_specs = (
        P(),
        P("ctx", "head"),
        P(None, "ctx"),
        P("ctx", "head", None),
        P("ctx", "head"),
        P(None, "ctx"),
    )
    out_specs = (P("ctx"), P("ctx", "head", None), P("ctx", "head"), P(("ctx", "head"), None))
    return jax.shard_map(body, mesh=mesh, in_specs=in_specs, out_specs=out_specs, check_vma=False)
```

time: 271 us -> 58.2 us (0.21)
  waiting for transfers between devices: 147 us -> 0 us
  Pallas kernels: 0 us -> 51.9 us
  blocking collectives: 40.2 us -> 0 us
  matrix products: 19.9 us -> 0 us
  starting transfers between devices: 18 us -> 0 us
  local copies, waits for them, and re-layouts: 21.6 us -> 5.44 us
  between operations: 15.3 us -> 0.64 us
  other arithmetic: 8.01 us -> 0 us
    reduce_scatter x1 -> x0, waiting for transfers between devices: 112 us -> none  [body(): lax.psum_scatter(stored_grad, ('ctx', 'head'), scatter_dimension=0, tiled...]
    pallas_call x0 -> x1, Pallas kernels: none -> 51.9 us  [body(): pl.pallas_call(functools.partial(kernel, (ctx_count, head_axis, block_row...]
    all_to_all x5 -> x0, waiting for transfers between devices: 35.1 us -> none  [the longest x1 24 us: body(): lax.all_to_all(main_query, 'head', split_axis=0, concat_axis=1, tiled=True)]
    all_gather x1 -> x0, blocking collectives: 32 us -> none  [body(): lax.all_gather(index_key, 'ctx', axis=1, tiled=True)]
    all_to_all x5 -> x0, starting transfers between devices: 17.9 us -> none  [the longest x1 4.24 us: body(): lax.all_to_all(index_weight, 'head', split_axis=0, concat_axis=1, tiled=T...]
    div x8 -> x0, matrix products: 14.4 us -> none  [causal_target(): raised / jnp.sum(raised, axis=2, keepdims=True)]
    unnamed x1 -> x0, blocking collectives: 8.12 us -> none
    all_to_all x8 -> x0, local copies, waits for them, and re-layouts: 5.56 us -> none  [the longest x1 3.26 us: body(): lax.all_to_all(main_query, 'head', split_axis=0, concat_axis=1, tiled=True)]
  transfers between devices with their start and end apart: 7 -> 0, of which waited for: 4 -> 0; matrix products, arithmetic and copies ran while one was open for 9% -> 0% of each run, Pallas kernels for 0% -> 0%
where the time goes in v1:
time: 58.2 us; the launch traced here: 58 us
  Pallas kernels  51.9 us (89%)
  local copies, waits for them, and re-layouts  5.44 us (9%)
  between operations  0.64 us (1%)
    pallas_call x1, Pallas kernels, body(): pl.pallas_call(functools.partial(kernel, (ctx_count, head_axis, block_row...  51.9 us
    unnamed x4, local copies, waits for them, and re-layouts  5.44 us

profile of v1, /device:TPU:0, one launch (start us, length us, event | category | flops | bytes accessed | tf_op | source)
XLA Modules:
  0.0 58.0 jit_solution(14503049965709110293)
XLA Ops:
  0.6 51.9 %shard_map.93 = (f32[1,128]{1,0:T(1,128)}, bf16[1024,128]{1,0:T(8,128)(2,1)}, bf16[8,128]{1,0:T(8,128)(2,1)}, f32[32,128]{1,0:T(8,128)}) custom-call(s32[16]{0:T(128)} %order_ref.1, bf16[128,9216]{1,0:T(8,128)(2,1)} %query_ref.1, bf16[576,128]{1,0:T(8,128)(2,1)} %latent_ref.1, bf16[1024,128]{1,0:T(8,128)(2,1)} %bitcast.6, bf16[8,128]{1,0:T(8,128)(2,1)} %bitcast.8, ...), custom_call_target="tpu_custom_call" | custom-call | tf_op jit(solution)/shard_map/pallas_call | solution.py:454
  52.5 1.2 %copy.14 = f32[128]{0:T(128)} copy(f32[128]{0:T(128)} %bitcast.9) | data formatting | bytes 1024
  53.7 1.7 %copy.15 = bf16[128,8,128]{2,1,0:T(8,128)(2,1)} copy(bf16[128,8,128]{2,1,0:T(8,128)(2,1)} %bitcast.5) | data formatting | bytes 524288
  55.4 1.3 %copy.16 = bf16[128,8]{0,1:T(8,128)(2,1)} copy(bf16[128,8]{0,1:T(8,128)(2,1)} %bitcast.7) | data formatting | bytes 4096
  56.7 1.3 %copy.17 = f32[32,128]{1,0:T(8,128)} copy(f32[32,128]{1,0:T(8,128)} %get-tuple-element.19) | data formatting | bytes 32768

commit v2 on v1

--- a/solution.py
+++ b/solution.py
@@ -36,15 +36,18 @@
     dims,
     order_ref,
     query_ref,
-    latent_ref,
-    rows_ref,
+    latent_in,
+    rows_in,
     weight_ref,
-    index_ref,
+    index_in,
     loss_ref,
     grad_rows_ref,
     grad_weight_ref,
     grad_key_ref,
     query_vmem,
+    rows_ref,
+    through_early,
+    through_late,
     all_latent,
     all_index,
     window_latent,
@@ -67,6 +70,7 @@
     key_send,
     got_piece,
     query_sem,
+    input_sem,
     index_send,
     index_recv,
     latent_send,
@@ -95,6 +99,13 @@
     beside = head + 1 - 2 * (head % 2)
 
     fetch_query = pltpu.make_async_copy(query_ref, query_vmem, query_sem)
+    fetch_inputs = [
+        pltpu.make_async_copy(index_in, all_index.at[me], input_sem.at[0]),
+        pltpu.make_async_copy(latent_in, all_latent.at[me], input_sem.at[1]),
+        pltpu.make_async_copy(rows_in, rows_ref, input_sem.at[2]),
+    ]
+    for fetch in fetch_inputs:
+        fetch.start()
     fetch_query.start()
 
     barrier = pltpu.get_barrier_semaphore()
@@ -123,17 +134,15 @@
             device_id_type=pl.DeviceIdType.MESH,
         )
 
-    def keys_plan(own_ref, all_ref, sends, recvs):
-        depth = own_ref.shape[0] // head_axis
+    def keys_plan(all_ref, sends, recvs):
+        depth = all_ref.shape[1] // head_axis
 
         def piece(owner, quarter_index):
             return all_ref.at[owner, pl.ds(pl.multiple_of(quarter_index * depth, 16), depth), :]
 
         def first(offset):
-            mine = own_ref.at[pl.ds(pl.multiple_of(head * depth, 16), depth), :]
-            return send(
-                mine, piece(me, head), sends.at[0, offset], recvs.at[0, offset], {"ctx": (me + offset) % ctx_count}
-            )
+            where = {"ctx": (me + offset) % ctx_count}
+            return send(piece(me, head), piece(me, head), sends.at[0, offset], recvs.at[0, offset], where)
 
         def onward(stage, offset):
             owner = (me + ctx_count - offset) % ctx_count
@@ -145,13 +154,13 @@
 
         return first, onward
 
-    index_first, index_onward = keys_plan(index_ref, all_index, index_send, index_recv)
-    latent_first, latent_onward = keys_plan(latent_ref, all_latent, latent_send, latent_recv)
+    index_first, index_onward = keys_plan(all_index, index_send, index_recv)
+    latent_first, latent_onward = keys_plan(all_latent, latent_send, latent_recv)
+    fetch_inputs[0].wait()
     each(1, ctx_count, lambda k: index_first(k).start())
+    fetch_inputs[1].wait()
     each(1, ctx_count, lambda k: latent_first(k).start())
-
-    all_index[me] = index_ref[...]
-    all_latent[me] = latent_ref[...]
+    fetch_inputs[2].wait()
 
     sequence = order_ref[2 * me] // ctx_count
     inner = order_ref[2 * me] % ctx_count
@@ -181,23 +190,18 @@
     window_latent[0:HALF, :] = jnp.zeros((HALF, length), jnp.bfloat16)
     window_latent[HALF + width :, :] = jnp.zeros((HALF, length), jnp.bfloat16)
 
-    def forward(onward):
-        def one(offset):
-            onward(0, offset).wait_recv()
-            onward(1, offset).start()
-            onward(2, offset).start()
-
-        def two(offset):
-            onward(1, offset).wait_recv()
-            onward(3, offset).start()
-
-        def three(offset):
-            onward(2, offset).wait_recv()
-            onward(3, offset).wait_recv()
-
-        each(1, ctx_count, one)
-        each(1, ctx_count, two)
-        each(1, ctx_count, three)
+    def pass_first(onward, offset):
+        onward(0, offset).wait_recv()
+        onward(1, offset).start()
+        onward(2, offset).start()
+
+    def pass_second(onward, offset):
+        onward(1, offset).wait_recv()
+        onward(3, offset).start()
+
+    def take_last(onward, offset):
+        onward(2, offset).wait_recv()
+        onward(3, offset).wait_recv()
 
     def arrange(all_ref, window_ref, top, depth):
         for pair in range(0, pairs, 2):
@@ -211,10 +215,10 @@
     chunk_rows = 16
     flat = chunk_rows * index_heads
     chunks = block_rows // chunk_rows
-    sides = ((0, early, 0, act_early), (1, length, early, act_late))
+    sides = ((0, early, 0, act_early, through_early), (1, length, early, act_late, through_late))
 
     def logits_of():
-        for side, columns, column_at, act_ref in sides:
+        for side, columns, column_at, act_ref, unused in sides:
 
             def chunk(i, carry):
                 local = pl.multiple_of(i * flat, flat)
@@ -254,7 +258,7 @@
         for parity in range(2):
             top = HALF if parity == 0 else 0
             lane_at = 0 if parity == 0 else width - HALF
-            for side, columns, column_at, unused in sides:
+            for side, columns, column_at, unused, unused in sides:
                 visible = visible_of(side, block_rows, 0, columns)
 
                 def run(i, carry):
@@ -279,11 +283,15 @@
 
                 lax.fori_loop(0, groups, run, 0)
 
-    forward(index_onward)
-    arrange(all_index, window_index, 0, index_ref.shape[0])
+    each(1, ctx_count, lambda k: pass_first(index_onward, k))
+    each(1, ctx_count, lambda k: pass_first(latent_onward, k))
+    each(1, ctx_count, lambda k: pass_second(index_onward, k))
+    each(1, ctx_count, lambda k: take_last(index_onward, k))
+    arrange(all_index, window_index, 0, window_index.shape[0])
     logits_of()
     each(1, head_axis, lambda k: share(part_logit, got_logit, logit_send, logit_recv, k).start())
-    forward(latent_onward)
+    each(1, ctx_count, lambda k: pass_second(latent_onward, k))
+    each(1, ctx_count, lambda k: take_last(latent_onward, k))
     arrange(all_latent, window_latent, HALF, width)
     fetch_query.wait()
     attention()
@@ -292,7 +300,7 @@
     each(1, head_axis, lambda k: share(part_target, got_target, target_send, target_recv, k).wait_recv())
 
     my_rows = pl.ds(pl.multiple_of(head * quarter, quarter), quarter)
-    for side, columns, column_at, unused in sides:
+    for side, columns, column_at, unused, unused in sides:
         at = slice(column_at, column_at + columns)
         visible = visible_of(side, quarter, head * quarter, columns)
         logit = part_logit[my_rows, at]
@@ -333,33 +341,49 @@
     key_turned[...] = jnp.zeros(key_turned.shape, jnp.float32)
     lane_of = lax.broadcasted_iota(jnp.int32, (flat, LANES), 1)
     lane_own = lane_of == lax.broadcasted_iota(jnp.int32, (flat, LANES), 0) % index_heads
-    for side, columns, column_at, act_ref in sides:
+    def slope_of(rows_at, column_at, columns):
+        slope = slopes[pl.ds(rows_at, chunk_rows), column_at : column_at + columns].astype(jnp.float32)
+        return jnp.broadcast_to(slope[:, None, :], (chunk_rows, index_heads, columns)).reshape(flat, columns)
+
+    for side, columns, column_at, act_ref, through_ref in sides:
 
         def chunk(i, carry):
             local = pl.multiple_of(i * flat, flat)
             at = pl.multiple_of(side * block_rows * index_heads + i * flat, flat)
             rows_at = pl.multiple_of(i * chunk_rows, chunk_rows)
             act = act_ref[pl.ds(local, flat), :]
-            slope = slopes[pl.ds(rows_at, chunk_rows), column_at : column_at + columns].astype(jnp.float32)
-            slope = jnp.broadcast_to(slope[:, None, :], (chunk_rows, index_heads, columns)).reshape(flat, columns)
-            col = jnp.sum(slope * jnp.maximum(act, 0.0), axis=1, keepdims=True)
-            placed = jnp.where(lane_own, col, 0.0).reshape(chunk_rows, index_heads, LANES)
-            weight_at = pl.multiple_of(side * block_rows + i * chunk_rows, chunk_rows)
-            weight_grads[pl.ds(weight_at, chunk_rows), :] = jnp.sum(placed, axis=1)
+            slope = slope_of(rows_at, column_at, columns)
             through = jnp.where(act > 0.0, slope * weight_col[pl.ds(at, flat), 0:1], 0.0).astype(jnp.bfloat16)
-            grad_rows_ref[pl.ds(at, flat), :] = lax.dot_general(
-                through,
-                window_index[:, 0:columns],
-                (((1,), (1,)), ((), ())),
-                preferred_element_type=jnp.float32,
-            ).astype(jnp.bfloat16)
+            through_ref[pl.ds(local, flat), :] = through
             key_turned[:, 0:columns] += dot(rows_turned[:, pl.ds(at, flat)], through)
             return carry
 
         lax.fori_loop(0, chunks, chunk, 0)
 
+    def row_grads():
+        for side, columns, column_at, act_ref, through_ref in sides:
+
+            def chunk(i, carry):
+                local = pl.multiple_of(i * flat, flat)
+                at = pl.multiple_of(side * block_rows * index_heads + i * flat, flat)
+                rows_at = pl.multiple_of(i * chunk_rows, chunk_rows)
+                slope = slope_of(rows_at, column_at, columns)
+                col = jnp.sum(slope * jnp.maximum(act_ref[pl.ds(local, flat), :], 0.0), axis=1, keepdims=True)
+                placed = jnp.where(lane_own, col, 0.0).reshape(chunk_rows, index_heads, LANES)
+                weight_at = pl.multiple_of(side * block_rows + i * chunk_rows, chunk_rows)
+                weight_grads[pl.ds(weight_at, chunk_rows), :] = jnp.sum(placed, axis=1)
+                grad_rows_ref[pl.ds(at, flat), :] = lax.dot_general(
+                    through_ref[pl.ds(local, flat), :],
+                    window_index[:, 0:columns],
+                    (((1,), (1,)), ((), ())),
+                    preferred_element_type=jnp.float32,
+                ).astype(jnp.bfloat16)
+                return carry
+
+            lax.fori_loop(0, chunks, chunk, 0)
+        grad_weight_ref[...] = weight_grads[...].T[0:index_heads].astype(jnp.bfloat16)
+
     slot_rows = 2 * block_rows // head_axis
-    grad_weight_ref[...] = weight_grads[...].T[0:index_heads].astype(jnp.bfloat16)
     for pair in range(pairs):
         low = pair * block_rows
         high = length - (pair + 1) * block_rows
@@ -377,6 +401,7 @@
         )
 
     each(1, head_axis, lambda k: share_key(k).start())
+    row_grads()
     each(1, head_axis, lambda k: spread_losses(k).wait_recv())
     loss_block = jnp.concatenate(
         [losses[q, side] for side in range(2) for q in range(head_axis)], axis=0
@@ -431,6 +456,12 @@
 
     each(1, ctx_count, finish_ctx)
     each(1, head_axis, finish_head)
+
+
+def hand_over(*refs):
+    count = len(refs) // 2
+    for source, target in zip(refs[:count], refs[count:]):
+        target[...] = source[...]
 
 
 def body(block_order, main_query, latent_key, index_query, index_weight, index_key):
@@ -450,8 +481,9 @@
     flat_rows = local_rows * index_heads
     f32, bf16 = jnp.float32, jnp.bfloat16
     vmem = pl.BlockSpec(memory_space=pltpu.VMEM)
+    hbm = pl.BlockSpec(memory_space=pl.ANY)
     dma = pltpu.SemaphoreType.DMA
-    loss, grad_rows, grad_weight, grad_key = pl.pallas_call(
+    results = pl.pallas_call(
         functools.partial(kernel, (ctx_count, head_axis, block_rows, heads, width, index_heads)),
         out_shape=(
             jax.ShapeDtypeStruct((1, local_rows), f32),
@@ -461,15 +493,18 @@
         ),
         in_specs=[
             pl.BlockSpec(memory_space=pltpu.SMEM),
-            pl.BlockSpec(memory_space=pl.ANY),
+            hbm,
+            hbm,
+            hbm,
             vmem,
-            vmem,
-            vmem,
-            vmem,
+            hbm,
         ],
         out_specs=(vmem, vmem, vmem, vmem),
         scratch_shapes=[
             pltpu.VMEM(main_query.shape, bf16),
+            pltpu.VMEM((flat_rows, index_width), bf16),
+            pltpu.VMEM((flat_rows // 2, early), bf16),
+            pltpu.VMEM((flat_rows // 2, length), bf16),
             pltpu.VMEM((ctx_count,) + latent_key.shape, bf16),
             pltpu.VMEM((ctx_count,) + index_key.shape, bf16),
             pltpu.VMEM((width + 2 * HALF, length), bf16),
@@ -492,6 +527,7 @@
             pltpu.VMEM((ctx_count, slot_rows, index_width), f32),
             pltpu.VMEM((ctx_count, slot_rows, index_width), f32),
             dma,
+            dma((3,)),
             dma((4, ctx_count)),
             dma((4, ctx_count)),
             dma((4, ctx_count)),
@@ -510,6 +546,12 @@
         index_weight.T,
         index_key,
     )
+    loss, grad_rows, grad_weight, grad_key = pl.pallas_call(
+        hand_over,
+        out_shape=tuple(jax.ShapeDtypeStruct(result.shape, result.dtype) for result in results),
+        in_specs=[vmem] * len(results),
+        out_specs=(vmem,) * len(results),
+    )(*results)
     return (
         loss.reshape(local_rows),
         grad_rows.reshape(local_rows, index_heads, index_width),

time: 58.2 us -> 47.7 us (0.82)
  local copies, waits for them, and re-layouts: 5.44 us -> 0 us
  Pallas kernels: 51.9 us -> 46.8 us
    pallas_call x1, Pallas kernels: 51.9 us -> 45.1 us  [body(): pl.pallas_call(functools.partial(kernel, (ctx_count, head_axis, block_row...]
    unnamed x4 -> x0, local copies, waits for them, and re-layouts: 5.44 us -> none
    pallas_call x0 -> x1, Pallas kernels: none -> 1.68 us  [body(): pl.pallas_call(hand_over, out_shape=tuple((jax.ShapeDtypeStruct(result.sh...]
where the time goes in v2:
time: 47.7 us; the launch traced here: 47.4 us
  Pallas kernels  46.8 us (98%)
  between operations  0.64 us (1%)
    pallas_call x1, Pallas kernels, body(): pl.pallas_call(functools.partial(kernel, (ctx_count, head_axis, block_row...  45.1 us
    pallas_call x1, Pallas kernels, body(): pl.pallas_call(hand_over, out_shape=tuple((jax.ShapeDtypeStruct(result.sh...  1.68 us

profile of v2, /device:TPU:0, one launch (start us, length us, event | category | flops | bytes accessed | tf_op | source)
XLA Modules:
  0.0 47.4 jit_solution(9480594799577462118)
XLA Ops:
  0.6 45.1 %shard_map.93 = (f32[1,128]{1,0:T(1,128)}, bf16[1024,128]{1,0:T(8,128)(2,1)}, bf16[8,128]{1,0:T(8,128)(2,1)}, f32[32,128]{1,0:T(8,128)}) custom-call(s32[16]{0:T(128)} %order_ref.1, bf16[128,9216]{1,0:T(8,128)(2,1)} %query_ref.1, bf16[576,128]{1,0:T(8,128)(2,1)} %latent_in.1, bf16[1024,128]{1,0:T(8,128)(2,1)} %bitcast.5, bf16[8,128]{1,0:T(8,128)(2,1)} %bitcast.6, ...), custom_call_target="tpu_custom_call" | custom-call | tf_op jit(solution)/shard_map/pallas_call | solution.py:486
  45.7 1.7 %shard_map.94 = (f32[1,128]{1,0:T(1,128)}, bf16[1024,128]{1,0:T(8,128)(2,1)}, bf16[8,128]{1,0:T(8,128)(2,1)}, f32[32,128]{1,0:T(8,128)}) custom-call(f32[1,128]{1,0:T(1,128)} %get-tuple-element.12.refs_0_, bf16[1024,128]{1,0:T(8,128)(2,1)} %get-tuple-element.13.refs_1_, bf16[8,128]{1,0:T(8,128)(2,1)} %get-tuple-element.14.refs_2_, ...), custom_call_target="tpu_custom_call" | custom-call | tf_op jit(solution)/shard_map/pallas_call | solution.py:549

commit v3 on v2

--- a/solution.py
+++ b/solution.py
@@ -284,13 +284,20 @@
                 lax.fori_loop(0, groups, run, 0)
 
     each(1, ctx_count, lambda k: pass_first(index_onward, k))
-    each(1, ctx_count, lambda k: pass_first(latent_onward, k))
+    lag = min(3, ctx_count - 1)
+    each(1, 1 + lag, lambda k: pass_first(latent_onward, k))
     each(1, ctx_count, lambda k: pass_second(index_onward, k))
+
+    def pass_both(offset):
+        pass_first(latent_onward, offset)
+        pass_second(latent_onward, offset - lag)
+
+    each(1 + lag, ctx_count, pass_both)
     each(1, ctx_count, lambda k: take_last(index_onward, k))
     arrange(all_index, window_index, 0, window_index.shape[0])
     logits_of()
     each(1, head_axis, lambda k: share(part_logit, got_logit, logit_send, logit_recv, k).start())
-    each(1, ctx_count, lambda k: pass_second(latent_onward, k))
+    each(ctx_count - lag, ctx_count, lambda k: pass_second(latent_onward, k))
     each(1, ctx_count, lambda k: take_last(latent_onward, k))
     arrange(all_latent, window_latent, HALF, width)
     fetch_query.wait()
@@ -392,7 +399,7 @@
             turned = key_turned[:, lanes_at : lanes_at + LANES].T
             for k in range(2):
                 begin = start - lanes_at + k * slot_rows
-                key_parts[part + k, pair] = turned[begin : begin + slot_rows]
+                key_parts[part + k, pair] = turned[begin : begin + slot_rows].astype(jnp.bfloat16)
 
     def share_key(offset):
         peer = (head + offset) % head_axis
@@ -412,15 +419,15 @@
     loss_ref[...] = jnp.sum(jnp.where(diagonal, loss_block, 0.0), axis=0, keepdims=True)
     each(1, head_axis, lambda k: share_key(k).wait_recv())
     for pair in range(pairs):
-        piece = key_parts[head, pair]
+        piece = key_parts[head, pair].astype(jnp.float32)
         for k in range(1, head_axis):
-            piece = piece + got_key[k, pair]
+            piece = piece + got_key[k, pair].astype(jnp.float32)
         key_piece[pair] = piece
 
     def fill(d):
         block = order_ref[2 * d]
         same = block // ctx_count == sequence
-        key_send[d] = jnp.where(same, key_piece[block % ctx_count], 0.0)
+        key_send[d] = jnp.where(same, key_piece[block % ctx_count], 0.0).astype(jnp.bfloat16)
 
     each(0, ctx_count, fill)
 
@@ -431,11 +438,11 @@
         )
 
     each(1, ctx_count, lambda k: share_piece(k).start())
-    grad_key_ref[...] = key_send[me]
+    grad_key_ref[...] = key_piece[inner]
 
     def add(offset):
         share_piece(offset).wait_recv()
-        grad_key_ref[...] += got_piece[offset]
+        grad_key_ref[...] += got_piece[offset].astype(jnp.float32)
 
     each(1, ctx_count, add)
 
@@ -521,11 +528,11 @@
             pltpu.VMEM((head_axis, 2, quarter, LANES), f32),
             pltpu.VMEM((local_rows, LANES), f32),
             pltpu.VMEM((index_width, length), f32),
-            pltpu.VMEM((head_axis, pairs, slot_rows, index_width), f32),
-            pltpu.VMEM((head_axis, pairs, slot_rows, index_width), f32),
+            pltpu.VMEM((head_axis, pairs, slot_rows, index_width), bf16),
+            pltpu.VMEM((head_axis, pairs, slot_rows, index_width), bf16),
             pltpu.VMEM((pairs, slot_rows, index_width), f32),
-            pltpu.VMEM((ctx_count, slot_rows, index_width), f32),
-            pltpu.VMEM((ctx_count, slot_rows, index_width), f32),
+            pltpu.VMEM((ctx_count, slot_rows, index_width), bf16),
+            pltpu.VMEM((ctx_count, slot_rows, index_width), bf16),
             dma,
             dma((3,)),
             dma((4, ctx_count)),

time: 47.7 us -> 47.6 us (level)
  no operation moved by 1% of the time
where the time goes in v3:
time: 47.6 us; the launch traced here: 47.4 us
  Pallas kernels  46.8 us (98%)
  between operations  0.64 us (1%)
    pallas_call x1, Pallas kernels, body(): pl.pallas_call(functools.partial(kernel, (ctx_count, head_axis, block_row...  45.1 us
    pallas_call x1, Pallas kernels, body(): pl.pallas_call(hand_over, out_shape=tuple((jax.ShapeDtypeStruct(result.sh...  1.68 us

profile of v3, /device:TPU:0, one launch (start us, length us, event | category | flops | bytes accessed | tf_op | source)
XLA Modules:
  0.0 47.4 jit_solution(8696486356874880832)
XLA Ops:
  0.6 45.1 %shard_map.93 = (f32[1,128]{1,0:T(1,128)}, bf16[1024,128]{1,0:T(8,128)(2,1)}, bf16[8,128]{1,0:T(8,128)(2,1)}, f32[32,128]{1,0:T(8,128)}) custom-call(s32[16]{0:T(128)} %order_ref.1, bf16[128,9216]{1,0:T(8,128)(2,1)} %query_ref.1, bf16[576,128]{1,0:T(8,128)(2,1)} %latent_in.1, bf16[1024,128]{1,0:T(8,128)(2,1)} %bitcast.5, bf16[8,128]{1,0:T(8,128)(2,1)} %bitcast.6, ...), custom_call_target="tpu_custom_call" | custom-call | tf_op jit(solution)/shard_map/pallas_call | solution.py:493
  45.8 1.7 %shard_map.94 = (f32[1,128]{1,0:T(1,128)}, bf16[1024,128]{1,0:T(8,128)(2,1)}, bf16[8,128]{1,0:T(8,128)(2,1)}, f32[32,128]{1,0:T(8,128)}) custom-call(f32[1,128]{1,0:T(1,128)} %get-tuple-element.12.refs_0_, bf16[1024,128]{1,0:T(8,128)(2,1)} %get-tuple-element.13.refs_1_, bf16[8,128]{1,0:T(8,128)(2,1)} %get-tuple-element.14.refs_2_, ...), custom_call_target="tpu_custom_call" | custom-call | tf_op jit(solution)/shard_map/pallas_call | solution.py:556

commit v4 on v3

--- a/solution.py
+++ b/solution.py
@@ -284,20 +284,13 @@
                 lax.fori_loop(0, groups, run, 0)
 
     each(1, ctx_count, lambda k: pass_first(index_onward, k))
-    lag = min(3, ctx_count - 1)
-    each(1, 1 + lag, lambda k: pass_first(latent_onward, k))
+    each(1, ctx_count, lambda k: pass_first(latent_onward, k))
     each(1, ctx_count, lambda k: pass_second(index_onward, k))
-
-    def pass_both(offset):
-        pass_first(latent_onward, offset)
-        pass_second(latent_onward, offset - lag)
-
-    each(1 + lag, ctx_count, pass_both)
     each(1, ctx_count, lambda k: take_last(index_onward, k))
     arrange(all_index, window_index, 0, window_index.shape[0])
     logits_of()
     each(1, head_axis, lambda k: share(part_logit, got_logit, logit_send, logit_recv, k).start())
-    each(ctx_count - lag, ctx_count, lambda k: pass_second(latent_onward, k))
+    each(1, ctx_count, lambda k: pass_second(latent_onward, k))
     each(1, ctx_count, lambda k: take_last(latent_onward, k))
     arrange(all_latent, window_latent, HALF, width)
     fetch_query.wait()

time: 47.6 us -> 46.7 us (0.981)
  Pallas kernels: 46.8 us -> 45.9 us
    pallas_call x1, Pallas kernels: 45.1 us -> 44.2 us  [body(): pl.pallas_call(functools.partial(kernel, (ctx_count, head_axis, block_row...]
where the time goes in v4:
time: 46.7 us; the launch traced here: 46.5 us
  Pallas kernels  45.9 us (98%)
  between operations  0.64 us (1%)
    pallas_call x1, Pallas kernels, body(): pl.pallas_call(functools.partial(kernel, (ctx_count, head_axis, block_row...  44.2 us
    pallas_call x1, Pallas kernels, body(): pl.pallas_call(hand_over, out_shape=tuple((jax.ShapeDtypeStruct(result.sh...  1.68 us

profile of v4, /device:TPU:0, one launch (start us, length us, event | category | flops | bytes accessed | tf_op | source)
XLA Modules:
  0.0 46.5 jit_solution(1488311784161566747)
XLA Ops:
  0.6 44.2 %shard_map.93 = (f32[1,128]{1,0:T(1,128)}, bf16[1024,128]{1,0:T(8,128)(2,1)}, bf16[8,128]{1,0:T(8,128)(2,1)}, f32[32,128]{1,0:T(8,128)}) custom-call(s32[16]{0:T(128)} %order_ref.1, bf16[128,9216]{1,0:T(8,128)(2,1)} %query_ref.1, bf16[576,128]{1,0:T(8,128)(2,1)} %latent_in.1, bf16[1024,128]{1,0:T(8,128)(2,1)} %bitcast.5, bf16[8,128]{1,0:T(8,128)(2,1)} %bitcast.6, ...), custom_call_target="tpu_custom_call" | custom-call | tf_op jit(solution)/shard_map/pallas_call | solution.py:486
  44.9 1.7 %shard_map.94 = (f32[1,128]{1,0:T(1,128)}, bf16[1024,128]{1,0:T(8,128)(2,1)}, bf16[8,128]{1,0:T(8,128)(2,1)}, f32[32,128]{1,0:T(8,128)}) custom-call(f32[1,128]{1,0:T(1,128)} %get-tuple-element.12.refs_0_, bf16[1024,128]{1,0:T(8,128)(2,1)} %get-tuple-element.13.refs_1_, bf16[8,128]{1,0:T(8,128)(2,1)} %get-tuple-element.14.refs_2_, ...), custom_call_target="tpu_custom_call" | custom-call | tf_op jit(solution)/shard_map/pallas_call | solution.py:549
